TPU v7x, 32 devices: a whole 2x2x4 slice. The times are simulated.
32 devices in a mesh: grp: 2 (over y), freq: 4 (over z), beam: 2 (over x), dm: 2 (over core).
Axes of the slice: x: 2, y: 2, z: 4, core: 2. Of those that a mesh axis runs over, the one named last changes fastest.
Arguments:
- voltages: bfloat16 [4, 2048, 16, 2, 1024], P(None, ('freq', 'beam'), ('grp', 'dm')), parts along dimension 2, may hold values from -6 to 6
- grid_feed: int32 [1024], replicated, may hold values from 0 to 1023, each once
- delays: int32 [4, 2048, 256], P('freq', None, 'dm'), may hold values from 0 to 4
Outputs:
- dedispersed: float32 [4, 256, 8, 1024], P('freq', 'dm', 'grp', 'beam'), parts along dimension 2
There are 2 independent parts, one for each index of `grp`. A program takes and returns all parts, laid end to end along the dimension named above; an argument that names none is the same for every part. Nothing has to cross between parts.
Inputs may be any that keep to these rules, and one draw needn't show every extreme that they name: `grid_feed`: each feed appears once.
All inputs are finite; a program needn't handle non-finite values.
Results may differ from a plain program's by a relative error of at most 0.0034.
Values may be sent and summed in bfloat16 or wider, within the bound.
A program may use at most 128 MiB of HBM per device.

v0:
```python
import math
import jax
import jax.numpy as jnp
from jax import lax
from jax.sharding import PartitionSpec as P

GX = 4
GY = 256
FREQS = 8192


def steering_table(length, factor):
    position = jnp.arange(length, dtype=jnp.int32)
    phase_step = position[:, None] * position[None, :] % length
    phase_angle = phase_step.astype(jnp.float32) * (2.0 * math.pi / length)
    cosine = jnp.cos(phase_angle) * factor
    sine_part = jnp.sin(phase_angle) * factor
    upper_half = jnp.concatenate([cosine, -sine_part], axis=1)
    lower_half = jnp.concatenate([sine_part, cosine], axis=1)
    return jnp.concatenate([upper_half, lower_half], axis=0).astype(jnp.bfloat16)


def quarter_table():
    position = jnp.arange(GX, dtype=jnp.int32)
    phase_step = position[:, None] * position[None, :] % GX
    cosine = jnp.where(phase_step == 0, 1.0, jnp.where(phase_step == 2, -1.0, 0.0)) * 0.5
    sine_part = jnp.where(phase_step == 1, 1.0, jnp.where(phase_step == 3, -1.0, 0.0)) * 0.5
    real_in = jnp.stack([cosine, -sine_part], axis=2)
    imag_in = jnp.stack([sine_part, cosine], axis=2)
    return jnp.stack([real_in, imag_in], axis=1).astype(jnp.float32)


def form_power(voltages, grid_feed):
    row_count = voltages.shape[0] * voltages.shape[1] * voltages.shape[2]
    feed_count = voltages.shape[4]
    gridded = jnp.take(voltages.reshape(row_count, 2, feed_count), grid_feed, axis=2)
    gridded = jnp.transpose(gridded.reshape(row_count, 2, GX, GY), (0, 2, 1, 3)).reshape(
        row_count * GX, 2 * GY
    )
    along_y = jnp.dot(
        gridded, steering_table(GY, 1.0 / math.sqrt(GY)), preferred_element_type=jnp.float32
    ).astype(jnp.bfloat16)
    along_y = along_y.reshape(row_count, GX, 2, GY).astype(jnp.float32)
    formed = jnp.einsum(
        "rgpy,gpbq->rbqy", along_y, quarter_table(), precision=lax.Precision.HIGHEST
    )
    intensity = 0.5 * (formed[:, :, 0, :] ** 2 + formed[:, :, 1, :] ** 2)
    return intensity.astype(jnp.bfloat16).reshape(row_count, feed_count)


def body(voltages, grid_feed, delays):
    band_count, sub_local, time_local = (voltages.shape[0], voltages.shape[1], voltages.shape[2])
    feed_count = voltages.shape[4]
    columns = lax.axis_size("beam")
    col_width = feed_count // columns
    intensity = form_power(voltages, grid_feed).reshape(
        band_count, sub_local, time_local, columns, col_width
    )
    regrouped = jnp.transpose(intensity, (0, 3, 1, 2, 4)).reshape(
        band_count * columns, sub_local, time_local, col_width
    )
    turned = lax.all_to_all(regrouped, ("freq", "beam"), split_axis=0, concat_axis=1, tiled=True)
    turned = turned.reshape(-1, time_local, col_width)
    full_time = lax.all_gather(turned, "dm", axis=1, tiled=True)
    sub_count, total_time = (full_time.shape[0], full_time.shape[1])
    levels = full_time.astype(jnp.float32)
    centered = (levels - jnp.mean(levels, axis=1, keepdims=True)).astype(jnp.bfloat16)
    flattened = centered.reshape(sub_count * total_time, col_width)
    out_time = total_time // 2
    offsets = jnp.arange(out_time, dtype=jnp.int32)
    sample_ids = jnp.arange(total_time, dtype=jnp.int32)
    dm_local = delays.shape[2]
    dm_block = 32
    lag_blocks = jnp.transpose(delays[0]).reshape(dm_local // dm_block, dm_block, sub_count)

    def dedisperse(lag_rows):
        shifted = offsets[None, :, None] + lag_rows[:, None, :]
        selector = (shifted[:, :, :, None] == sample_ids[None, None, None, :]).astype(jnp.bfloat16)
        summed = jnp.dot(
            selector.reshape(dm_block * out_time, sub_count * total_time),
            flattened,
            preferred_element_type=jnp.float32,
        )
        return summed.reshape(dm_block, out_time, col_width)

    partial_sum = lax.map(dedisperse, lag_blocks).reshape(dm_local, out_time, col_width)
    cumulative = lax.all_to_all(
        jnp.cumsum(
            lax.all_to_all(partial_sum[None], "freq", split_axis=1, concat_axis=0, tiled=True),
            axis=0,
        ),
        "freq",
        split_axis=0,
        concat_axis=1,
        tiled=True,
    )
    return cumulative * (1.0 / math.sqrt(FREQS))


def solution(mesh):
    in_specs = (P(None, ("freq", "beam"), ("grp", "dm"), None, None), P(), P("freq", None, "dm"))
    out_specs = P("freq", "dm", "grp", "beam")
    return jax.shard_map(body, mesh=mesh, in_specs=in_specs, out_specs=out_specs, check_vma=False)
```

profile of v0, /device:TPU:0, one launch (start us, length us, event | category | flops | bytes accessed | tf_op | source)
XLA Modules:
  0.0 787.1 jit_solution(15443421244380062521)
XLA Ops:
  6.5 0.0 all-gather.2.cloned.1.call-start
  6.6 1.1 negate_convert_fusion
  7.7 0.7 fusion.43
  8.4 0.7 compare_and_fusion
  9.1 1.0 fusion.40
  10.1 0.1 copy.58
  10.2 0.1 copy.59
  10.3 56.0 %copy.60 = bf16[4096,2,1024]{0,1,2:T(2,128)(2,1)} copy(bf16[4096,2,1024]{2,1,0:T(2,128)(2,1)} %bitcast.78) | data formatting | bytes 33554432 | tf_op jit(solution)/shard_map/reshape | solution.py:36
  66.3 66.2 %gather_fusion = bf16[1024,4096,2]{1,2,0:T(2,128)(2,1)} fusion(bf16[4096,2,1024]{0,1,2:T(2,128)(2,1)} %copy.60, s32[1024]{0:T(1024)S(1)} %fusion.43), kind=kCustom, calls=%fused_computation | custom fusion | bytes 33558528 | tf_op jit(solution)/shard_map/jit(_take)/gather | solution.py:36
  132.5 56.3 %copy.61 = bf16[4096,2,4,256]{3,1,2,0:T(2,128)(2,1)} copy(bf16[4096,2,4,256]{0,1,3,2:T(2,128)(2,1)} %bitcast.75) | data formatting | bytes 33554432 | tf_op jit(solution)/shard_map/jit(_take)/gather | solution.py:36
  188.8 16.6 %broadcast_select_fusion = bf16[4096,2,4,256]{3,1,2,0:T(2,128)(2,1)S(1)} fusion(bf16[4096,2,4,256]{3,1,2,0:T(2,128)(2,1)} %copy.61, pred[4,256]{1,0:T(4,128)(4,1)S(1)} %broadcast_in_dim.47), kind=kLoop, calls=%fused_computation.15 | loop fusion | flops 8388608 | bytes 33555456 | tf_op jit(solution)/shard_map/jit(_take)/select_n | solution.py:36
  205.4 10.7 %copy.80 = bf16[2048,8,2,256]{3,1,2,0:T(8,128)(2,1)} copy(bf16[2048,8,2,256]{3,2,1,0:T(2,128)(2,1)S(1)} %bitcast.74) | data formatting | bytes 33554432
  216.0 20.0 %convolution_convert_fusion = bf16[16384,512]{1,0:T(8,128)(2,1)} fusion(bf16[16384,512]{1,0:T(8,128)(2,1)} %bitcast.79, bf16[256,256]{1,0:T(8,128)(2,1)S(1)} %get-tuple-element.76, bf16[256,256]{1,0:T(8,128)(2,1)S(1)} %fusion.40, bf16[256,256]{1,0:T(8,128)(2,1)S(1)} %get-tuple-element.75), kind=kOutput, calls=%fused_computation.16 | convolution fusion | flops 8600420352 | bytes 33947648 | tf_op jit(solution)/shard_map/dot_general | solution.py:40
  236.1 23.9 %reshape.188 = bf16[4096,4,2,256]{3,2,1,0:T(2,128)(2,1)} reshape(bf16[16384,512]{1,0:T(8,128)(2,1)} %convolution_convert_fusion) | data formatting | bytes 33554432 | tf_op jit(solution)/shard_map/reshape | solution.py:43
  259.9 45.2 %fusion.22 = f32[4096,4,2,256]{3,1,0,2:T(4,128)} fusion(bf16[4096,4,2,256]{3,2,1,0:T(2,128)(2,1)} %reshape.188, f32[4,1,4,2]{0,2,1,3:T(4,128)S(1)} %copy.59, f32[4,1,4,2]{0,2,1,3:T(4,128)S(1)} %copy.58), kind=kOutput, calls=%fused_computation.26 | convolution fusion | flops 805306432 | bytes 50331904 | tf_op jit(solution)/shard_map/rgpy,gpbq->rbqy/dot_general | solution.py:44
  305.1 16.6 %fusion.18 = bf16[4096,4,1,256]{3,1,0,2:T(4,128)(2,1)} fusion(f32[4096,4,2,256]{3,1,0,2:T(4,128)} %fusion.22), kind=kLoop, calls=%fused_computation.21 | loop fusion | flops 20971520 | bytes 41943040 | tf_op jit(solution)/shard_map/convert_element_type | solution.py:48
  321.7 18.1 %convert_element_type.31 = bf16[4,256,4,2,512]{4,3,2,1,0:T(2,128)(2,1)} reshape(bf16[4096,4,1,256]{3,1,0,2:T(4,128)(2,1)} %fusion.18) | data formatting | bytes 16777216 | tf_op jit(solution)/shard_map/convert_element_type | solution.py:48
  339.8 9.8 %copy.63 = bf16[4,256,4,2,512]{4,1,2,3,0:T(8,128)(2,1)} copy(bf16[4,256,4,2,512]{4,3,2,1,0:T(2,128)(2,1)} %convert_element_type.31) | data formatting | bytes 16777216 | tf_op jit(solution)/shard_map/convert_element_type | solution.py:48
  349.6 190.6 %all_to_all.30 = bf16[8,256,4,512]{3,1,2,0:T(8,128)(2,1)} all-to-all(bf16[8,256,4,512]{3,1,2,0:T(8,128)(2,1)} %bitcast.77), channel_id=1, replica_groups=mesh['grp'=2,'freq'=4,'beam'=2,'dm'=2] {'freq','beam'}, dimensions={0} | all-to-all | bytes 16777216 | tf_op jit(solution)/shard_map/all_to_all | solution.py:62
  540.3 0.0 copy-start.1
  540.3 7.6 copy.64
  547.8 0.0 all-gather.2.cloned.1.call-update
  547.9 0.0 copy-done.1
  547.9 0.3 copy.57
  548.2 29.0 %all-gather.2.cloned.1.call-done = bf16[2048,8,512]{2,0,1:T(8,128)(2,1)} async-done(((bf16[2048,4,512]{2,0,1:T(8,128)(2,1)}), bf16[2048,8,512]{2,0,1:T(8,128)(2,1)}) %all-gather.2.cloned.1.call-update) | async-done | bytes 16777232 | tf_op jit(solution)/shard_map/all_gather | solution.py:64
  577.2 0.0 copy-start
  577.2 20.3 %convert_reduce_fusion = f32[2048,512]{1,0:T(8,128)S(1)} fusion(bf16[2048,8,512]{2,0,1:T(8,128)(2,1)} %all-gather.2.cloned.1.call-done), kind=kLoop, calls=%fused_computation.13 | loop fusion | flops 15728640 | bytes 20971520 | tf_op jit(solution)/shard_map/reduce_sum | solution.py:67
  597.6 0.5 broadcast_multiply_fusion
  598.1 0.0 copy-done
  598.1 43.1 %fusion.15 = bf16[16384,512]{1,0:T(8,128)(2,1)} fusion(f32[2048,512]{1,0:T(8,128)S(1)} %broadcast_multiply_fusion, bf16[2048,8,512]{2,0,1:T(8,128)(2,1)S(1)} %copy-done), kind=kLoop, calls=%fused_computation.17 | loop fusion | flops 25165824 | bytes 37748736 | tf_op jit(solution)/shard_map/reshape | solution.py:68
  641.2 76.5 %while.11 = (s32[]{:T(128)}, f32[4,32,4,512]{3,1,0,2:T(8,128)S(1)}, s32[4,32,2048]{2,1,0:T(8,128)S(1)}, bf16[16384,512]{1,0:T(8,128)(2,1)}, s32[]{:T(128)}) while((s32[]{:T(128)}, f32[4,32,4,512]{3,1,0,2:T(8,128)S(1)}, s32[4,32,2048]{2,1,0:T(8,128)S(1)}, bf16[16384,512]{1,0:T(8,128)(2,1)}, s32[]{:T(128)}) %tuple.33), condition=%wide.region_2.3_spmd.clone, body=%wide.region_1.2_spmd.clone.sunk | while | flops 2149842944 | bytes 20709444 | solution.py:86
  641.2 0.3 copy.93
  641.5 2.2 iota_add_fusion.2
  643.8 0.1 iota.55
  643.8 0.5 eq.131
  644.3 15.9 %fusion.52 = f32[4,32,4,512]{3,1,0,2:T(8,128)S(1)} fusion(f32[4,32,4,512]{3,1,0,2:T(8,128)S(1)} %get-tuple-element.110, s32[]{:T(128)} %get-tuple-element.109, bf16[16384,512]{1,0:T(8,128)(2,1)} %get-tuple-element.117, s32[16384]{0:T(1024)S(1)} %eq.131, s32[32,4,2048]{0,2,1:T(8,128)} %iota_add_fusion.2), kind=kOutput, calls=%fused_computation.10.clone.1 | convolution fusion | flops 2149580800 | bytes 18153476 | tf_op jit(solution)/shard_map/while/body/eval_jaxpr/dot_general | solution.py:79
  660.3 0.3 copy.93
  660.7 2.2 iota_add_fusion.2
  662.9 0.1 iota.55
  663.0 0.5 eq.131
  663.5 16.0 %fusion.52 = f32[4,32,4,512]{3,1,0,2:T(8,128)S(1)} fusion(f32[4,32,4,512]{3,1,0,2:T(8,128)S(1)} %get-tuple-element.110, s32[]{:T(128)} %get-tuple-element.109, bf16[16384,512]{1,0:T(8,128)(2,1)} %get-tuple-element.117, s32[16384]{0:T(1024)S(1)} %eq.131, s32[32,4,2048]{0,2,1:T(8,128)} %iota_add_fusion.2), kind=kOutput, calls=%fused_computation.10.clone.1 | convolution fusion | flops 2149580800 | bytes 18153476 | tf_op jit(solution)/shard_map/while/body/eval_jaxpr/dot_general | solution.py:79
  679.5 0.3 copy.93
  679.8 2.2 iota_add_fusion.2
  682.0 0.1 iota.55
  682.1 0.5 eq.131
  682.6 16.0 %fusion.52 = f32[4,32,4,512]{3,1,0,2:T(8,128)S(1)} fusion(f32[4,32,4,512]{3,1,0,2:T(8,128)S(1)} %get-tuple-element.110, s32[]{:T(128)} %get-tuple-element.109, bf16[16384,512]{1,0:T(8,128)(2,1)} %get-tuple-element.117, s32[16384]{0:T(1024)S(1)} %eq.131, s32[32,4,2048]{0,2,1:T(8,128)} %iota_add_fusion.2), kind=kOutput, calls=%fused_computation.10.clone.1 | convolution fusion | flops 2149580800 | bytes 18153476 | tf_op jit(solution)/shard_map/while/body/eval_jaxpr/dot_general | solution.py:79
  698.6 0.3 copy.93
  699.0 2.2 iota_add_fusion.2
  701.2 0.1 iota.55
  701.3 0.5 eq.131
  701.8 16.0 %fusion.52 = f32[4,32,4,512]{3,1,0,2:T(8,128)S(1)} fusion(f32[4,32,4,512]{3,1,0,2:T(8,128)S(1)} %get-tuple-element.110, s32[]{:T(128)} %get-tuple-element.109, bf16[16384,512]{1,0:T(8,128)(2,1)} %get-tuple-element.117, s32[16384]{0:T(1024)S(1)} %eq.131, s32[32,4,2048]{0,2,1:T(8,128)} %iota_add_fusion.2), kind=kOutput, calls=%fused_computation.10.clone.1 | convolution fusion | flops 2149580800 | bytes 18153476 | tf_op jit(solution)/shard_map/while/body/eval_jaxpr/dot_general | solution.py:79
  717.7 0.7 copy.68
  718.4 30.8 %all_to_all.31 = f32[1,128,4,512]{3,2,0,1:T(4,128)S(1)} all-to-all(f32[1,128,4,512]{3,2,0,1:T(4,128)S(1)} %copy.68), channel_id=1, replica_groups=mesh['grp'=2,'freq'=4,'beam'=2,'dm'=2] {'freq'}, dimensions={1} | all-to-all | bytes 2097152 | tf_op jit(solution)/shard_map/all_to_all | solution.py:89
  749.3 0.9 fusion.25
  750.2 27.9 %all_to_all.32 = f32[4,32,4,512]{3,1,2,0:T(8,128)S(1)} all-to-all(f32[4,32,4,512]{3,1,2,0:T(8,128)S(1)} %fusion.25), channel_id=1, replica_groups=mesh['grp'=2,'freq'=4,'beam'=2,'dm'=2] {'freq'}, dimensions={0} | all-to-all | bytes 2097152 | tf_op jit(solution)/shard_map/all_to_all | solution.py:87
  778.1 0.2 copy_multiply_fusion
  778.2 1.6 copy.71
  (9 shorter events, 0.1 us)
Async XLA Ops:
  6.5 570.7 %all-gather.2.cloned.1.call-start = ((), (), s32[]{:S(2)}) async-start(), calls=%async_computation.3 | async-start | bytes 25165824 | tf_op jit(solution)/shard_map/all_gather | solution.py:64
  540.3 7.6 copy-start.1
  577.2 20.8 %copy-start = (bf16[2048,8,512]{2,0,1:T(8,128)(2,1)S(1)}, bf16[2048,8,512]{2,0,1:T(8,128)(2,1)}, u32[]{:S(2)}) copy-start(bf16[2048,8,512]{2,0,1:T(8,128)(2,1)} %all-gather.2.cloned.1.call-done) | copy-start | bytes 50331652
Sparse Core Ops, SparseCore 0:
  548.0 29.1 all-gather.1
where the time goes:
time: 800 us; the launch traced here: 787 us
  local copies, waits for them, and re-layouts  255 us (32%)
  blocking collectives  249 us (31%)
  matrix products  129 us (16%)
  other arithmetic  111 us (14%)
  waiting for transfers between devices  29 us (4%)
  between operations  13.9 us (2%)
    all_to_all x1, blocking collectives, body(): lax.all_to_all(regrouped, ('freq', 'beam'), split_axis=0, concat_axis=1,...  191 us
    gather x2, local copies, waits for them, and re-layouts, form_power(): jnp.take(voltages.reshape(row_count, 2, feed_count), grid_feed, axis=2)  122 us
    dot_general x4, matrix products, dedisperse(): jnp.dot(selector.reshape(dm_block * out_time, sub_count * total_time), fl...  63.8 us
    reshape x1, local copies, waits for them, and re-layouts, form_power(): voltages.reshape(row_count, 2, feed_count)  56 us
    dot_general x1, matrix products, form_power(): jnp.einsum('rgpy,gpbq->rbqy', along_y, quarter_table(), precision=lax.Pre...  45.2 us
    reshape x1, other arithmetic, body(): flattened = centered.reshape(sub_count * total_time, col_width)  43.1 us
    all_to_all x1, blocking collectives, body(): lax.all_to_all(partial_sum[None], 'freq', split_axis=1, concat_axis=0, ti...  30.8 us
    all_gather x1, waiting for transfers between devices, body(): full_time = lax.all_gather(turned, 'dm', axis=1, tiled=True)  29 us
  transfers between devices with their start and end apart: 1, of which 1 were waited for; matrix products, arithmetic and copies ran while one was open for 0% of the time, Pallas kernels for 0%

commit v1 on v0

--- a/solution.py
+++ b/solution.py
@@ -7,6 +7,17 @@
 GX = 4
 GY = 256
 FREQS = 8192
+
+
+def split_up(x, dim, size):
+    before, after = (x.shape[:dim], x.shape[dim + 1 :])
+    return jnp.moveaxis(x.reshape(*before, size, -1, *after), dim, 0)
+
+
+def joined_along(parts, dim):
+    parts = jnp.moveaxis(parts, 0, dim)
+    dims = parts.shape
+    return parts.reshape(*dims[:dim], dims[dim] * dims[dim + 1], *dims[dim + 2 :])
 
 
 def steering_table(length, factor):
@@ -84,16 +95,18 @@
         return summed.reshape(dm_block, out_time, col_width)
 
     partial_sum = lax.map(dedisperse, lag_blocks).reshape(dm_local, out_time, col_width)
-    cumulative = lax.all_to_all(
-        jnp.cumsum(
-            lax.all_to_all(partial_sum[None], "freq", split_axis=1, concat_axis=0, tiled=True),
-            axis=0,
-        ),
-        "freq",
-        split_axis=0,
-        concat_axis=1,
-        tiled=True,
+    array = jnp.cumsum(
+        lax.all_to_all(partial_sum[None], "freq", split_axis=1, concat_axis=0, tiled=True), axis=0
     )
+    size, index = (lax.axis_size("freq"), lax.axis_index("freq"))
+    tiles = split_up(array, 0, size)
+    filled = tiles
+    for step in range(1, size):
+        target, source = ((index + step) % size, (index - step) % size)
+        sent = lax.dynamic_index_in_dim(tiles, target, 0)
+        other = lax.ppermute(sent, "freq", [(i, (i + step) % size) for i in range(size)])
+        filled = lax.dynamic_update_slice_in_dim(filled, other, source, axis=0)
+    cumulative = joined_along(filled, 1)
     return cumulative * (1.0 / math.sqrt(FREQS))
 
 

time: 800 us -> 795 us (level)
  blocking collectives: 249 us -> 191 us
  waiting for transfers between devices: 29 us -> 71.9 us
  starting transfers between devices: 0.01 us -> 8.74 us
    all_to_all x2 -> x0, blocking collectives: 58.7 us -> none  [the longest x1 30.8 us: body(): lax.all_to_all(partial_sum[None], 'freq', split_axis=1, concat_axis=0, ti...]
    all_to_all x0 -> x1, waiting for transfers between devices: none -> 26.2 us  [body(): lax.all_to_all(partial_sum[None], 'freq', split_axis=1, concat_axis=0, ti...]
    ppermute x0 -> x3, waiting for transfers between devices: none -> 16.7 us  [body(): lax.ppermute(sent, 'freq', [(i, (i + step) % size) for i in range(size)])]
  transfers between devices with their start and end apart: 1 -> 5, of which waited for: 1 -> 4; matrix products, arithmetic and copies ran while one was open for 0% -> 0% of each run, Pallas kernels for 0% -> 0%
where the time goes in v1:
time: 795 us; the launch traced here: 780 us
  local copies, waits for them, and re-layouts  255 us (32%)
  blocking collectives  191 us (24%)
  matrix products  129 us (16%)
  other arithmetic  111 us (14%)
  waiting for transfers between devices  71.9 us (9%)
  between operations  13.9 us (2%)
  starting transfers between devices  8.74 us (1%)
    all_to_all x1, blocking collectives, body(): lax.all_to_all(regrouped, ('freq', 'beam'), split_axis=0, concat_axis=1,...  191 us
    gather x2, local copies, waits for them, and re-layouts, form_power(): jnp.take(voltages.reshape(row_count, 2, feed_count), grid_feed, axis=2)  123 us
    dot_general x4, matrix products, dedisperse(): jnp.dot(selector.reshape(dm_block * out_time, sub_count * total_time), fl...  63.8 us
    reshape x1, local copies, waits for them, and re-layouts, form_power(): voltages.reshape(row_count, 2, feed_count)  56 us
    dot_general x1, matrix products, form_power(): jnp.einsum('rgpy,gpbq->rbqy', along_y, quarter_table(), precision=lax.Pre...  45.2 us
    reshape x1, other arithmetic, body(): flattened = centered.reshape(sub_count * total_time, col_width)  43.1 us
    all_gather x1, waiting for transfers between devices, body(): full_time = lax.all_gather(turned, 'dm', axis=1, tiled=True)  29 us
    convert_element_type x2, local copies, waits for them, and re-layouts, form_power(): return intensity.astype(jnp.bfloat16).reshape(row_count, feed_count)  28 us
  transfers between devices with their start and end apart: 5, of which 4 were waited for; matrix products, arithmetic and copies ran while one was open for 0% of the time, Pallas kernels for 0%

profile of v1, /device:TPU:0, one launch (start us, length us, event | category | flops | bytes accessed | tf_op | source)
XLA Modules:
  0.0 780.0 jit_solution(11331995818257744149)
XLA Ops:
  6.5 0.0 all-gather.2.cloned.1.call-start
  6.6 1.1 negate_convert_fusion
  7.7 0.7 fusion.41
  8.4 0.7 compare_and_fusion
  9.1 1.0 fusion.38
  10.1 0.1 copy.44
  10.2 0.1 copy.45
  10.3 56.0 %copy.46 = bf16[4096,2,1024]{0,1,2:T(2,128)(2,1)} copy(bf16[4096,2,1024]{2,1,0:T(2,128)(2,1)} %bitcast.86) | data formatting | bytes 33554432 | tf_op jit(solution)/shard_map/reshape | solution.py:47
  66.3 66.3 %gather_fusion = bf16[1024,4096,2]{1,2,0:T(2,128)(2,1)} fusion(bf16[4096,2,1024]{0,1,2:T(2,128)(2,1)} %copy.46, s32[1024]{0:T(1024)S(1)} %fusion.41), kind=kCustom, calls=%fused_computation | custom fusion | bytes 33558528 | tf_op jit(solution)/shard_map/jit(_take)/gather | solution.py:47
  132.5 56.3 %copy.47 = bf16[4096,2,4,256]{3,1,2,0:T(2,128)(2,1)} copy(bf16[4096,2,4,256]{0,1,3,2:T(2,128)(2,1)} %bitcast.83) | data formatting | bytes 33554432 | tf_op jit(solution)/shard_map/jit(_take)/gather | solution.py:47
  188.9 16.6 %broadcast_select_fusion = bf16[4096,2,4,256]{3,1,2,0:T(2,128)(2,1)S(1)} fusion(bf16[4096,2,4,256]{3,1,2,0:T(2,128)(2,1)} %copy.47, pred[4,256]{1,0:T(4,128)(4,1)S(1)} %broadcast_in_dim.47), kind=kLoop, calls=%fused_computation.15 | loop fusion | flops 8388608 | bytes 33555456 | tf_op jit(solution)/shard_map/jit(_take)/select_n | solution.py:47
  205.4 10.7 %copy.63 = bf16[2048,8,2,256]{3,1,2,0:T(8,128)(2,1)} copy(bf16[2048,8,2,256]{3,2,1,0:T(2,128)(2,1)S(1)} %bitcast.82) | data formatting | bytes 33554432
  216.1 20.0 %convolution_convert_fusion = bf16[16384,512]{1,0:T(8,128)(2,1)} fusion(bf16[16384,512]{1,0:T(8,128)(2,1)} %bitcast.87, bf16[256,256]{1,0:T(8,128)(2,1)S(1)} %get-tuple-element.77, bf16[256,256]{1,0:T(8,128)(2,1)S(1)} %fusion.38, bf16[256,256]{1,0:T(8,128)(2,1)S(1)} %get-tuple-element.76), kind=kOutput, calls=%fused_computation.16 | convolution fusion | flops 8600420352 | bytes 33947648 | tf_op jit(solution)/shard_map/dot_general | solution.py:51
  236.2 23.9 %reshape.191 = bf16[4096,4,2,256]{3,2,1,0:T(2,128)(2,1)} reshape(bf16[16384,512]{1,0:T(8,128)(2,1)} %convolution_convert_fusion) | data formatting | bytes 33554432 | tf_op jit(solution)/shard_map/reshape | solution.py:54
  260.1 45.2 %fusion.22 = f32[4096,4,2,256]{3,1,0,2:T(4,128)} fusion(bf16[4096,4,2,256]{3,2,1,0:T(2,128)(2,1)} %reshape.191, f32[4,1,4,2]{0,2,1,3:T(4,128)S(1)} %copy.45, f32[4,1,4,2]{0,2,1,3:T(4,128)S(1)} %copy.44), kind=kOutput, calls=%fused_computation.26 | convolution fusion | flops 805306432 | bytes 50331904 | tf_op jit(solution)/shard_map/rgpy,gpbq->rbqy/dot_general | solution.py:55
  305.2 16.6 %fusion.18 = bf16[4096,4,1,256]{3,1,0,2:T(4,128)(2,1)} fusion(f32[4096,4,2,256]{3,1,0,2:T(4,128)} %fusion.22), kind=kLoop, calls=%fused_computation.21 | loop fusion | flops 20971520 | bytes 41943040 | tf_op jit(solution)/shard_map/convert_element_type | solution.py:59
  321.8 18.1 %convert_element_type.31 = bf16[4,256,4,2,512]{4,3,2,1,0:T(2,128)(2,1)} reshape(bf16[4096,4,1,256]{3,1,0,2:T(4,128)(2,1)} %fusion.18) | data formatting | bytes 16777216 | tf_op jit(solution)/shard_map/convert_element_type | solution.py:59
  340.0 9.8 %copy.49 = bf16[4,256,4,2,512]{4,1,2,3,0:T(8,128)(2,1)} copy(bf16[4,256,4,2,512]{4,3,2,1,0:T(2,128)(2,1)} %convert_element_type.31) | data formatting | bytes 16777216 | tf_op jit(solution)/shard_map/convert_element_type | solution.py:59
  349.8 190.6 %all_to_all.21 = bf16[8,256,4,512]{3,1,2,0:T(8,128)(2,1)} all-to-all(bf16[8,256,4,512]{3,1,2,0:T(8,128)(2,1)} %bitcast.85), channel_id=1, replica_groups=mesh['grp'=2,'freq'=4,'beam'=2,'dm'=2] {'freq','beam'}, dimensions={0} | all-to-all | bytes 16777216 | tf_op jit(solution)/shard_map/all_to_all | solution.py:73
  540.4 0.0 copy-start.1
  540.4 7.6 copy.50
  548.0 0.0 all-gather.2.cloned.1.call-update
  548.0 0.0 copy-done.1
  548.0 0.3 copy.43
  548.4 29.0 %all-gather.2.cloned.1.call-done = bf16[2048,8,512]{2,0,1:T(8,128)(2,1)} async-done(((bf16[2048,4,512]{2,0,1:T(8,128)(2,1)}), bf16[2048,8,512]{2,0,1:T(8,128)(2,1)}) %all-gather.2.cloned.1.call-update) | async-done | bytes 16777232 | tf_op jit(solution)/shard_map/all_gather | solution.py:75
  577.4 0.0 copy-start
  577.4 20.3 %convert_reduce_fusion = f32[2048,512]{1,0:T(8,128)S(1)} fusion(bf16[2048,8,512]{2,0,1:T(8,128)(2,1)} %all-gather.2.cloned.1.call-done), kind=kLoop, calls=%fused_computation.13 | loop fusion | flops 15728640 | bytes 20971520 | tf_op jit(solution)/shard_map/reduce_sum | solution.py:78
  597.7 0.5 broadcast_multiply_fusion
  598.2 0.0 copy-done
  598.2 43.1 %fusion.15 = bf16[16384,512]{1,0:T(8,128)(2,1)} fusion(f32[2048,512]{1,0:T(8,128)S(1)} %broadcast_multiply_fusion, bf16[2048,8,512]{2,0,1:T(8,128)(2,1)S(1)} %copy-done), kind=kLoop, calls=%fused_computation.17 | loop fusion | flops 25165824 | bytes 37748736 | tf_op jit(solution)/shard_map/reshape | solution.py:79
  641.3 76.5 %while.11 = (s32[]{:T(128)}, f32[4,32,4,512]{3,1,0,2:T(8,128)S(1)}, s32[4,32,2048]{2,1,0:T(8,128)S(1)}, bf16[16384,512]{1,0:T(8,128)(2,1)}, s32[]{:T(128)}) while((s32[]{:T(128)}, f32[4,32,4,512]{3,1,0,2:T(8,128)S(1)}, s32[4,32,2048]{2,1,0:T(8,128)S(1)}, bf16[16384,512]{1,0:T(8,128)(2,1)}, s32[]{:T(128)}) %tuple.34), condition=%wide.region_2.3_spmd.clone, body=%wide.region_1.2_spmd.clone.sunk | while | flops 2149842944 | bytes 20709444 | solution.py:97
  641.4 0.3 copy.73
  641.7 2.2 iota_add_fusion.2
  643.9 0.1 iota.55
  644.0 0.5 eq.138
  644.5 16.0 %fusion.52 = f32[4,32,4,512]{3,1,0,2:T(8,128)S(1)} fusion(f32[4,32,4,512]{3,1,0,2:T(8,128)S(1)} %get-tuple-element.109, s32[]{:T(128)} %get-tuple-element.108, bf16[16384,512]{1,0:T(8,128)(2,1)} %get-tuple-element.116, s32[16384]{0:T(1024)S(1)} %eq.138, s32[32,4,2048]{0,2,1:T(8,128)} %iota_add_fusion.2), kind=kOutput, calls=%fused_computation.10.clone.1 | convolution fusion | flops 2149580800 | bytes 18153476 | tf_op jit(solution)/shard_map/while/body/eval_jaxpr/dot_general | solution.py:90
  660.5 0.3 copy.73
  660.8 2.2 iota_add_fusion.2
  663.1 0.1 iota.55
  663.1 0.5 eq.138
  663.6 16.0 %fusion.52 = f32[4,32,4,512]{3,1,0,2:T(8,128)S(1)} fusion(f32[4,32,4,512]{3,1,0,2:T(8,128)S(1)} %get-tuple-element.109, s32[]{:T(128)} %get-tuple-element.108, bf16[16384,512]{1,0:T(8,128)(2,1)} %get-tuple-element.116, s32[16384]{0:T(1024)S(1)} %eq.138, s32[32,4,2048]{0,2,1:T(8,128)} %iota_add_fusion.2), kind=kOutput, calls=%fused_computation.10.clone.1 | convolution fusion | flops 2149580800 | bytes 18153476 | tf_op jit(solution)/shard_map/while/body/eval_jaxpr/dot_general | solution.py:90
  679.6 0.3 copy.73
  680.0 2.2 iota_add_fusion.2
  682.2 0.1 iota.55
  682.3 0.5 eq.138
  682.8 16.0 %fusion.52 = f32[4,32,4,512]{3,1,0,2:T(8,128)S(1)} fusion(f32[4,32,4,512]{3,1,0,2:T(8,128)S(1)} %get-tuple-element.109, s32[]{:T(128)} %get-tuple-element.108, bf16[16384,512]{1,0:T(8,128)(2,1)} %get-tuple-element.116, s32[16384]{0:T(1024)S(1)} %eq.138, s32[32,4,2048]{0,2,1:T(8,128)} %iota_add_fusion.2), kind=kOutput, calls=%fused_computation.10.clone.1 | convolution fusion | flops 2149580800 | bytes 18153476 | tf_op jit(solution)/shard_map/while/body/eval_jaxpr/dot_general | solution.py:90
  698.8 0.3 copy.73
  699.1 2.2 iota_add_fusion.2
  701.3 0.1 iota.55
  701.4 0.5 eq.138
  701.9 16.0 %fusion.52 = f32[4,32,4,512]{3,1,0,2:T(8,128)S(1)} fusion(f32[4,32,4,512]{3,1,0,2:T(8,128)S(1)} %get-tuple-element.109, s32[]{:T(128)} %get-tuple-element.108, bf16[16384,512]{1,0:T(8,128)(2,1)} %get-tuple-element.116, s32[16384]{0:T(1024)S(1)} %eq.138, s32[32,4,2048]{0,2,1:T(8,128)} %iota_add_fusion.2), kind=kOutput, calls=%fused_computation.10.clone.1 | convolution fusion | flops 2149580800 | bytes 18153476 | tf_op jit(solution)/shard_map/while/body/eval_jaxpr/dot_general | solution.py:90
  717.9 1.6 copy.54
  719.5 4.9 all-to-all-start.1
  724.4 26.2 %all-to-all-done.1 = f32[1,128,4,512]{3,2,0,1:T(4,128)S(1)} async-done(((f32[1,128,4,512]{3,2,0,1:T(4,128)}), f32[1,128,4,512]{3,2,0,1:T(4,128)S(1)}, u32[]{:S(2)}, u32[]{:S(2)}) %all-to-all-start.1) | async-done | bytes 1048608 | tf_op jit(solution)/shard_map/all_to_all | solution.py:99
  750.6 0.2 fusion.46
  750.8 0.1 dynamic-slice_bitcast_fusion
  750.8 0.1 collective-permute-start
  750.9 2.0 collective-permute-start.1
  752.9 1.8 collective-permute-start.2
  754.7 7.2 collective-permute-done
  762.0 9.4 %collective-permute-done.1 = f32[1,1,32,4,512]{4,3,2,0,1:T(4,128)S(1)} collective-permute-done((f32[1,1,32,4,512]{4,3,2,0,1:T(4,128)S(1)}, f32[1,1,32,4,512]{4,3,2,0,1:T(4,128)S(1)}, u32[]{:S(2)}, u32[]{:S(2)}) %collective-permute-start.1) | collective-permute-done | bytes 262176 | tf_op jit(solution)/shard_map/ppermute | solution.py:107
  771.5 0.0 collective-permute-done.2
  771.5 1.2 broadcast_multiply_fusion.1
  (12 shorter events, 0.2 us)
Async XLA Ops:
  6.5 570.9 %all-gather.2.cloned.1.call-start = ((), (), s32[]{:S(2)}) async-start(), calls=%async_computation.2 | async-start | bytes 25165824 | tf_op jit(solution)/shard_map/all_gather | solution.py:75
  540.4 7.6 copy-start.1
  577.4 20.8 %copy-start = (bf16[2048,8,512]{2,0,1:T(8,128)(2,1)S(1)}, bf16[2048,8,512]{2,0,1:T(8,128)(2,1)}, u32[]{:S(2)}) copy-start(bf16[2048,8,512]{2,0,1:T(8,128)(2,1)} %all-gather.2.cloned.1.call-done) | copy-start | bytes 50331652
  719.5 31.0 %all-to-all-start.1 = ((f32[1,128,4,512]{3,2,0,1:T(4,128)}), f32[1,128,4,512]{3,2,0,1:T(4,128)S(1)}, u32[]{:S(2)}, u32[]{:S(2)}) async-start(f32[1,128,4,512]{3,2,0,1:T(4,128)} %copy.54), calls=%async_computation.1 | async-start | bytes 2097152 | tf_op jit(solution)/shard_map/all_to_all | solution.py:99
  750.8 11.1 %collective-permute-start = (f32[1,1,32,4,512]{4,3,2,0,1:T(4,128)S(1)}, f32[1,1,32,4,512]{4,3,2,0,1:T(4,128)S(1)}, u32[]{:S(2)}, u32[]{:S(2)}) collective-permute-start(f32[1,1,32,4,512]{4,3,2,0,1:T(4,128)S(1)} %get-tuple-element.71), channel_id=1, source_target_pairs={{0,4},{4,8},{8,12},{12,0},{1,5},{5,9},{9,13},{13,1},{2,6},{6,10},{... | collective-permute-start | bytes 786440 | tf_op jit(solution)/shard_map/ppermute | solution.py:107
  750.9 20.5 %collective-permute-start.1 = (f32[1,1,32,4,512]{4,3,2,0,1:T(4,128)S(1)}, f32[1,1,32,4,512]{4,3,2,0,1:T(4,128)S(1)}, u32[]{:S(2)}, u32[]{:S(2)}) collective-permute-start(f32[1,1,32,4,512]{4,3,2,0,1:T(4,128)S(1)} %get-tuple-element.70), channel_id=1, source_target_pairs={{0,8},{4,12},{8,0},{12,4},{1,9},{5,13},{9,1},{13,5},{2,10},{6,14},... | collective-permute-start | bytes 786440 | tf_op jit(solution)/shard_map/ppermute | solution.py:107
  752.9 18.6 %collective-permute-start.2 = (f32[1,1,32,4,512]{4,3,2,0,1:T(4,128)S(1)}, f32[1,1,32,4,512]{4,3,2,0,1:T(4,128)S(1)}, u32[]{:S(2)}, u32[]{:S(2)}) collective-permute-start(f32[1,1,32,4,512]{4,3,2,0,1:T(4,128)S(1)} %get-tuple-element.69), channel_id=1, source_target_pairs={{0,12},{4,0},{8,4},{12,8},{1,13},{5,1},{9,5},{13,9},{2,14},{6,2},{... | collective-permute-start | bytes 786440 | tf_op jit(solution)/shard_map/ppermute | solution.py:107
Sparse Core Ops, SparseCore 0:
  548.1 29.2 all-gather.1
